TPU v7x, 32 devices: a whole 2x2x4 slice. The times are simulated.
32 devices in a mesh: row: 4 (over y, x), col: 8 (over z, core).
Axes of the slice: x: 2, y: 2, z: 4, core: 2. Of those that a mesh axis runs over, the one named last changes fastest.
Arguments:
- features: bfloat16 [8192, 512], P(('row', 'col')), may hold values from -6 to 6
- tile_values: bfloat16 [4, 8, 128, 128, 128], P('row', 'col'), may hold values from -0.1875 to 0.1875
- tile_places: int32 [4, 8, 2, 128], P('row', 'col'), may hold values from 0 to 15, as said below
- tile_counts: int32 [4, 8], replicated, may hold values from 40 to 128, as said below
- weight_one: float32 [512, 512], replicated, may hold values from -0.25 to 0.25
- weight_two: float32 [512, 512], replicated, may hold values from -0.25 to 0.25
Outputs:
- embedded: float32 [8192, 512], P(('row', 'col'))
Inputs may be any that keep to these rules, and one draw needn't show every extreme that they name: `tile_places`: in every block the first tile_counts slots name distinct tiles with tile rows below 16 and tile columns below 8, listed in order of tile row (never falling); later slots also name tiles in range. `tile_counts`: some block has exactly 128 tiles.
All inputs are finite; a program needn't handle non-finite values.
Results may differ from a plain program's by a relative error of at most 0.0029.
Values may be sent and summed in bfloat16 or wider, within the bound.
A program may use at most 64 MiB of HBM per device.

v0:
```python
import jax
import jax.numpy as jnp
from jax import lax
from jax.sharding import PartitionSpec as P

TR = 16


def add_slots(
    partial_value, blocks, row_ids, col_ids, column_tiles, first_slot, stop_slot, row_base
):
    slot_count = blocks.shape[0]
    group_size = min(16, slot_count)
    last_row = partial_value.shape[0] - 1

    def one_turn(group, totals):
        offset = jnp.minimum(group * group_size, slot_count - group_size)
        tile_group = lax.dynamic_slice_in_dim(blocks, offset, group_size, 0)
        group_rows = lax.dynamic_slice_in_dim(row_ids, offset, group_size, 0)
        group_cols = lax.dynamic_slice_in_dim(col_ids, offset, group_size, 0)
        positions = offset + jnp.arange(group_size, dtype=jnp.int32)
        active = (positions >= jnp.maximum(first_slot, group * group_size)) & (
            positions < stop_slot
        )
        products = jnp.einsum(
            "sij,sjf->sif", tile_group, column_tiles[group_cols], preferred_element_type=jnp.float32
        )
        products = jnp.where(active[:, None, None], products, 0.0)
        local_rows = jnp.clip(group_rows - row_base, 0, last_row)
        return totals.at[local_rows].add(products)

    first_turn = first_slot // group_size
    last_turn = (stop_slot + group_size - 1) // group_size
    return lax.fori_loop(first_turn, last_turn, one_turn, partial_value)


def shards(features, tile_values, tile_places, tile_counts, weight_one, weight_two):
    blocks = tile_values.reshape(tile_values.shape[2:])
    places = tile_places.reshape(tile_places.shape[2:])
    tile_size = blocks.shape[1]
    width_all = features.shape[1]
    block_row = lax.axis_index("row")
    block_col = lax.axis_index("col")
    own_count = tile_counts[block_row, block_col]

    def layer(inputs, weights):
        gathered = lax.all_gather(inputs, "row", axis=0, tiled=True)
        column_tiles = gathered.reshape(gathered.shape[0] // tile_size, tile_size, width_all)
        partial_value = jnp.zeros((TR, tile_size, width_all), jnp.float32)
        partial_value = add_slots(
            partial_value, blocks, places[0], places[1], column_tiles, 0, own_count, 0
        )
        mine = lax.psum_scatter(
            partial_value.reshape(TR * tile_size, width_all), "col", scatter_dimension=0, tiled=True
        )
        return jnp.maximum(jnp.dot(mine, weights, precision=lax.Precision.HIGHEST), 0.0)

    hidden = layer(features, weight_one).astype(jnp.bfloat16)
    return layer(hidden, weight_two)


def solution(mesh):
    placed = (
        P(("row", "col"), None),
        P("row", "col", None, None, None),
        P("row", "col", None, None),
        P(),
        P(),
        P(),
    )
    return jax.shard_map(
        shards, mesh=mesh, in_specs=placed, out_specs=P(("row", "col"), None), check_vma=False
    )
```

profile of v0, /device:TPU:0, one launch (start us, length us, event | category | flops | bytes accessed | tf_op | source)
XLA Modules:
  0.0 428.9 jit_solution(628005692319676586)
XLA Ops:
  6.5 0.7 all-gather.3.cloned.1.call-update
  7.3 1.3 dynamic_slice.21
  9.4 0.8 slice_bitcast_fusion
  10.1 28.3 %all-gather.3.cloned.1.call-done = bf16[1024,512]{1,0:T(8,128)(2,1)} async-done(((bf16[256,512]{1,0:T(8,128)(2,1)}), bf16[1024,512]{1,0:T(8,128)(2,1)}) %all-gather.3.cloned.1.call-update) | async-done | bytes 1048592 | tf_op jit(solution)/shard_map/all_gather | solution.py:47
  38.4 2.5 broadcast.45.clone
  41.0 91.4 %while.20 = (s32[]{:T(128)}, f32[16,128,512]{2,1,0:T(8,128)}, s32[]{:T(128)}, s32[128]{0:T(128)S(1)}, s32[]{:T(128)}, /*index=5*/bf16[128,128,128]{2,1,0:T(8,128...) while((s32[]{:T(128)}, f32[16,128,512]{2,1,0:T(8,128)}, ...), condition=%wide.region_2.3_spmd, body=%wide.region_0.2_spmd.sunk | while | flops 270533824 | bytes 23597752 | solution.py:34
  41.0 0.1 compare_select_fusion.6
  41.0 1.9 gather_fusion
  43.0 0.7 compare_and_fusion.4
  43.7 3.7 convolution_select_fusion.4
  47.3 8.8 %scatter_fusion = f32[16,128,512]{2,1,0:T(8,128)} fusion(f32[16,128,512]{2,1,0:T(8,128)} %get-tuple-element.253, s32[16]{0:T(128)S(1)} %get-tuple-element.227, f32[16,128,512]{2,1,0:T(8,128)} %convolution_select_fusion.4), kind=kCustom, calls=%fused_computation.2.clone.1 | custom fusion | flops 1048576 | bytes 12582976 | tf_op jit(solution)/shard_map/while/body/scatter-add | solution.py:30
  56.2 1.9 gather_fusion
  58.2 0.7 compare_and_fusion.4
  58.9 3.7 convolution_select_fusion.4
  62.5 8.8 %scatter_fusion = f32[16,128,512]{2,1,0:T(8,128)} fusion(f32[16,128,512]{2,1,0:T(8,128)} %get-tuple-element.253, s32[16]{0:T(128)S(1)} %get-tuple-element.227, f32[16,128,512]{2,1,0:T(8,128)} %convolution_select_fusion.4), kind=kCustom, calls=%fused_computation.2.clone.1 | custom fusion | flops 1048576 | bytes 12582976 | tf_op jit(solution)/shard_map/while/body/scatter-add | solution.py:30
  71.4 0.1 compare_select_fusion.6
  71.4 1.9 gather_fusion
  73.4 0.7 compare_and_fusion.4
  74.1 3.7 convolution_select_fusion.4
  77.7 8.7 %scatter_fusion = f32[16,128,512]{2,1,0:T(8,128)} fusion(f32[16,128,512]{2,1,0:T(8,128)} %get-tuple-element.253, s32[16]{0:T(128)S(1)} %get-tuple-element.227, f32[16,128,512]{2,1,0:T(8,128)} %convolution_select_fusion.4), kind=kCustom, calls=%fused_computation.2.clone.1 | custom fusion | flops 1048576 | bytes 12582976 | tf_op jit(solution)/shard_map/while/body/scatter-add | solution.py:30
  86.5 1.9 gather_fusion
  88.4 0.7 compare_and_fusion.4
  89.1 3.7 convolution_select_fusion.4
  92.8 8.9 %scatter_fusion = f32[16,128,512]{2,1,0:T(8,128)} fusion(f32[16,128,512]{2,1,0:T(8,128)} %get-tuple-element.253, s32[16]{0:T(128)S(1)} %get-tuple-element.227, f32[16,128,512]{2,1,0:T(8,128)} %convolution_select_fusion.4), kind=kCustom, calls=%fused_computation.2.clone.1 | custom fusion | flops 1048576 | bytes 12582976 | tf_op jit(solution)/shard_map/while/body/scatter-add | solution.py:30
  101.7 0.1 compare_select_fusion.6
  101.8 1.9 gather_fusion
  103.7 0.7 compare_and_fusion.4
  104.4 3.7 convolution_select_fusion.4
  108.1 8.9 %scatter_fusion = f32[16,128,512]{2,1,0:T(8,128)} fusion(f32[16,128,512]{2,1,0:T(8,128)} %get-tuple-element.253, s32[16]{0:T(128)S(1)} %get-tuple-element.227, f32[16,128,512]{2,1,0:T(8,128)} %convolution_select_fusion.4), kind=kCustom, calls=%fused_computation.2.clone.1 | custom fusion | flops 1048576 | bytes 12582976 | tf_op jit(solution)/shard_map/while/body/scatter-add | solution.py:30
  117.1 1.9 gather_fusion
  119.0 0.7 compare_and_fusion.4
  119.7 3.7 convolution_select_fusion.4
  123.4 9.0 %scatter_fusion = f32[16,128,512]{2,1,0:T(8,128)} fusion(f32[16,128,512]{2,1,0:T(8,128)} %get-tuple-element.253, s32[16]{0:T(128)S(1)} %get-tuple-element.227, f32[16,128,512]{2,1,0:T(8,128)} %convolution_select_fusion.4), kind=kCustom, calls=%fused_computation.2.clone.1 | custom fusion | flops 1048576 | bytes 12582976 | tf_op jit(solution)/shard_map/while/body/scatter-add | solution.py:30
  132.5 82.7 %reduce-scatter.3.cloned.1.call-done = f32[256,512]{1,0:T(8,128)} async-done(((f32[2048,512]{1,0:T(8,128)}), f32[256,512]{1,0:T(8,128)}) %reduce-scatter.3.cloned.1.call-update) | async-done | bytes 524304 | tf_op jit(solution)/shard_map/reduce_scatter | solution.py:53
  215.2 2.8 fusion.4
  218.1 25.1 %all-gather.5.cloned.1.call-done = bf16[1024,512]{1,0:T(8,128)(2,1)} async-done(((bf16[256,512]{1,0:T(8,128)(2,1)}), bf16[1024,512]{1,0:T(8,128)(2,1)}) %all-gather.5.cloned.1.call-update) | async-done | bytes 1048592 | tf_op jit(solution)/shard_map/all_gather | solution.py:47
  243.1 2.5 broadcast.45
  245.6 91.7 %while.21 = (s32[]{:T(128)}, f32[16,128,512]{2,1,0:T(8,128)}, s32[]{:T(128)}, s32[128]{0:T(128)S(1)}, s32[]{:T(128)}, /*index=5*/bf16[128,128,128]{2,1,0:T(8,128...) while((s32[]{:T(128)}, f32[16,128,512]{2,1,0:T(8,128)}, ...), condition=%wide.region_6.7_spmd, body=%wide.region_4.6_spmd.sunk | while | flops 270533824 | bytes 23597752 | solution.py:34
  245.7 1.9 gather_fusion.1
  247.6 0.7 compare_and_fusion.5
  248.3 3.7 convolution_select_fusion.5
  252.0 9.1 %scatter_fusion.1 = f32[16,128,512]{2,1,0:T(8,128)} fusion(f32[16,128,512]{2,1,0:T(8,128)} %get-tuple-element.292, s32[16]{0:T(128)S(1)} %get-tuple-element.237, f32[16,128,512]{2,1,0:T(8,128)} %convolution_select_fusion.5), kind=kCustom, calls=%fused_computation.3.clone.1 | custom fusion | flops 1048576 | bytes 12582976 | tf_op jit(solution)/shard_map/while/body/scatter-add | solution.py:30
  261.2 1.9 gather_fusion.1
  263.1 0.7 compare_and_fusion.5
  263.8 3.7 convolution_select_fusion.5
  267.5 8.8 %scatter_fusion.1 = f32[16,128,512]{2,1,0:T(8,128)} fusion(f32[16,128,512]{2,1,0:T(8,128)} %get-tuple-element.292, s32[16]{0:T(128)S(1)} %get-tuple-element.237, f32[16,128,512]{2,1,0:T(8,128)} %convolution_select_fusion.5), kind=kCustom, calls=%fused_computation.3.clone.1 | custom fusion | flops 1048576 | bytes 12582976 | tf_op jit(solution)/shard_map/while/body/scatter-add | solution.py:30
  276.4 1.9 gather_fusion.1
  278.3 0.7 compare_and_fusion.5
  279.0 3.7 convolution_select_fusion.5
  282.8 8.8 %scatter_fusion.1 = f32[16,128,512]{2,1,0:T(8,128)} fusion(f32[16,128,512]{2,1,0:T(8,128)} %get-tuple-element.292, s32[16]{0:T(128)S(1)} %get-tuple-element.237, f32[16,128,512]{2,1,0:T(8,128)} %convolution_select_fusion.5), kind=kCustom, calls=%fused_computation.3.clone.1 | custom fusion | flops 1048576 | bytes 12582976 | tf_op jit(solution)/shard_map/while/body/scatter-add | solution.py:30
  291.7 1.9 gather_fusion.1
  293.6 0.7 compare_and_fusion.5
  294.3 3.7 convolution_select_fusion.5
  298.0 8.8 %scatter_fusion.1 = f32[16,128,512]{2,1,0:T(8,128)} fusion(f32[16,128,512]{2,1,0:T(8,128)} %get-tuple-element.292, s32[16]{0:T(128)S(1)} %get-tuple-element.237, f32[16,128,512]{2,1,0:T(8,128)} %convolution_select_fusion.5), kind=kCustom, calls=%fused_computation.3.clone.1 | custom fusion | flops 1048576 | bytes 12582976 | tf_op jit(solution)/shard_map/while/body/scatter-add | solution.py:30
  306.9 1.9 gather_fusion.1
  308.8 0.7 compare_and_fusion.5
  309.5 3.7 convolution_select_fusion.5
  313.2 8.8 %scatter_fusion.1 = f32[16,128,512]{2,1,0:T(8,128)} fusion(f32[16,128,512]{2,1,0:T(8,128)} %get-tuple-element.292, s32[16]{0:T(128)S(1)} %get-tuple-element.237, f32[16,128,512]{2,1,0:T(8,128)} %convolution_select_fusion.5), kind=kCustom, calls=%fused_computation.3.clone.1 | custom fusion | flops 1048576 | bytes 12582976 | tf_op jit(solution)/shard_map/while/body/scatter-add | solution.py:30
  322.1 1.9 gather_fusion.1
  324.0 0.7 compare_and_fusion.5
  324.7 3.7 convolution_select_fusion.5
  328.5 8.8 %scatter_fusion.1 = f32[16,128,512]{2,1,0:T(8,128)} fusion(f32[16,128,512]{2,1,0:T(8,128)} %get-tuple-element.292, s32[16]{0:T(128)S(1)} %get-tuple-element.237, f32[16,128,512]{2,1,0:T(8,128)} %convolution_select_fusion.5), kind=kCustom, calls=%fused_computation.3.clone.1 | custom fusion | flops 1048576 | bytes 12582976 | tf_op jit(solution)/shard_map/while/body/scatter-add | solution.py:30
  337.3 82.1 %reduce-scatter.5.cloned.1.call-done = f32[256,512]{1,0:T(8,128)} async-done(((f32[2048,512]{1,0:T(8,128)}), f32[256,512]{1,0:T(8,128)}) %reduce-scatter.5.cloned.1.call-update) | async-done | bytes 524304 | tf_op jit(solution)/shard_map/reduce_scatter | solution.py:53
  419.5 2.9 convolution_maximum_fusion
  (32 shorter events, 1.0 us)
Async XLA Ops:
  6.5 208.6 %copy-start = (f32[512,512]{1,0:T(8,128)S(1)}, f32[512,512]{1,0:T(8,128)}, u32[]{:S(2)}) copy-start(f32[512,512]{1,0:T(8,128)} %param.14) | copy-start | bytes 3145732
  6.5 31.9 %all-gather.3.cloned.1.call-start = ((), (), s32[]{:S(2)}) async-start(), calls=%async_computation.2 | async-start | bytes 1310720 | tf_op jit(solution)/shard_map/all_gather | solution.py:47
  7.3 207.9 %reduce-scatter.3.cloned.1.call-start = ((), (), s32[]{:S(2)}) async-start(), calls=%async_computation.3 | async-start | bytes 4718592 | tf_op jit(solution)/shard_map/reduce_scatter | solution.py:53
  132.4 110.7 %all-gather.5.cloned.1.call-start = ((), (), s32[]{:S(2)}) async-start(), calls=%async_computation.4 | async-start | bytes 1310720 | tf_op jit(solution)/shard_map/all_gather | solution.py:47
  218.0 201.5 %reduce-scatter.5.cloned.1.call-start = ((), (), s32[]{:S(2)}) async-start(), calls=%async_computation.5 | async-start | bytes 4718592 | tf_op jit(solution)/shard_map/reduce_scatter | solution.py:53
  337.3 82.2 %copy-start.1 = (f32[512,512]{1,0:T(8,128)S(1)}, f32[512,512]{1,0:T(8,128)}, u32[]{:S(2)}) copy-start(f32[512,512]{1,0:T(8,128)} %param.15) | copy-start | bytes 3145732
Sparse Core Ops, SparseCore 0:
  9.2 29.2 all-gather.2
  132.5 82.5 reduce-scatter.2
  218.1 24.9 all-gather.4
  337.4 81.9 reduce-scatter.4
where the time goes:
time: 431 us; the launch traced here: 429 us
  waiting for transfers between devices  219 us (51%)
  other arithmetic  116 us (27%)
  matrix products  50.2 us (12%)
  local copies, waits for them, and re-layouts  30 us (7%)
  between operations  13.9 us (3%)
    reduce_scatter x2, waiting for transfers between devices, layer(): lax.psum_scatter(partial_value.reshape(TR * tile_size, width_all), 'col',...  165 us
    scatter-add x12, other arithmetic, one_turn(): return totals.at[local_rows].add(products)  106 us
    all_gather x2, waiting for transfers between devices, layer(): gathered = lax.all_gather(inputs, 'row', axis=0, tiled=True)  53.4 us
    dot_general x12, matrix products, one_turn(): jnp.einsum('sij,sjf->sif', tile_group, column_tiles[group_cols], preferre...  44.5 us
    gather x12, local copies, waits for them, and re-layouts, one_turn(): column_tiles[group_cols]  22.9 us
  transfers between devices with their start and end apart: 4, of which 4 were waited for; matrix products, arithmetic and copies ran while one was open for 0% of the time, Pallas kernels for 0%

commit v1 on v0

--- a/solution.py
+++ b/solution.py
@@ -44,7 +44,18 @@
     own_count = tile_counts[block_row, block_col]
 
     def layer(inputs, weights):
-        gathered = lax.all_gather(inputs, "row", axis=0, tiled=True)
+
+        def link_bands_now(sample, a_name):
+            axis_total = lax.psum(1, a_name)
+            shelf = [(k, (k + 1) % axis_total) for k in range(axis_total)]
+            b_next = [None] * axis_total
+            b_next[axis_total - 1] = sample
+            for s in range(axis_total - 2, -1, -1):
+                b_next[s] = lax.ppermute(b_next[s + 1], a_name, shelf)
+            far_arr = jnp.concatenate(b_next, 0)
+            return jnp.roll(far_arr, (lax.axis_index(a_name) + 1) * sample.shape[0], 0)
+
+        gathered = link_bands_now(inputs, "row")
         column_tiles = gathered.reshape(gathered.shape[0] // tile_size, tile_size, width_all)
         partial_value = jnp.zeros((TR, tile_size, width_all), jnp.float32)
         partial_value = add_slots(

time: 431 us -> 436 us (1.012)
  waiting for transfers between devices: 219 us -> 204 us
  other arithmetic: 116 us -> 129 us
  starting transfers between devices: 0.12 us -> 7.51 us
    all_gather x2 -> x0, waiting for transfers between devices: 53.4 us -> none  [layer(): gathered = lax.all_gather(inputs, 'row', axis=0, tiled=True)]
    ppermute x0 -> x6, waiting for transfers between devices: none -> 38.7 us  [link_bands_now(): b_next[s] = lax.ppermute(b_next[s + 1], a_name, shelf)]
    concatenate x0 -> x2, other arithmetic: none -> 13.6 us  [link_bands_now(): return jnp.roll(far_arr, (lax.axis_index(a_name) + 1) * sample.shape[0], 0)]
    ppermute x0 -> x6, starting transfers between devices: none -> 7.47 us  [link_bands_now(): b_next[s] = lax.ppermute(b_next[s + 1], a_name, shelf)]
  transfers between devices with their start and end apart: 4 -> 8, of which waited for: 4 -> 8; matrix products, arithmetic and copies ran while one was open for 0% -> 0% of each run, Pallas kernels for 0% -> 0%
where the time goes in v1:
time: 436 us; the launch traced here: 434 us
  waiting for transfers between devices  204 us (47%)
  other arithmetic  129 us (30%)
  matrix products  49.2 us (11%)
  local copies, waits for them, and re-layouts  30 us (7%)
  between operations  14.1 us (3%)
  starting transfers between devices  7.51 us (2%)
    reduce_scatter x2, waiting for transfers between devices, layer(): lax.psum_scatter(partial_value.reshape(TR * tile_size, width_all), 'col',...  165 us
    scatter-add x12, other arithmetic, one_turn(): return totals.at[local_rows].add(products)  106 us
    dot_general x12, matrix products, one_turn(): jnp.einsum('sij,sjf->sif', tile_group, column_tiles[group_cols], preferre...  44.2 us
    ppermute x6, waiting for transfers between devices, link_bands_now(): b_next[s] = lax.ppermute(b_next[s + 1], a_name, shelf)  38.7 us
    gather x12, local copies, waits for them, and re-layouts, one_turn(): column_tiles[group_cols]  22.9 us
    concatenate x2, other arithmetic, link_bands_now(): return jnp.roll(far_arr, (lax.axis_index(a_name) + 1) * sample.shape[0], 0)  13.6 us
  transfers between devices with their start and end apart: 8, of which 8 were waited for; matrix products, arithmetic and copies ran while one was open for 0% of the time, Pallas kernels for 0%

profile of v1, /device:TPU:0, one launch (start us, length us, event | category | flops | bytes accessed | tf_op | source)
XLA Modules:
  0.0 433.9 jit_solution(4403239344351083126)
XLA Ops:
  6.5 3.0 collective-permute-start
  9.5 7.5 %collective-permute-done = bf16[256,512]{1,0:T(8,128)(2,1)S(1)} collective-permute-done((bf16[256,512]{1,0:T(8,128)(2,1)}, bf16[256,512]{1,0:T(8,128)(2,1)S(1)}, u32[]{:S(2)}, u32[]{:S(2)}) %collective-permute-start) | collective-permute-done | bytes 262176 | tf_op jit(solution)/shard_map/ppermute | solution.py:54
  17.0 0.8 collective-permute-start.1
  17.8 7.6 %collective-permute-done.1 = bf16[256,512]{1,0:T(8,128)(2,1)S(1)} collective-permute-done((bf16[256,512]{1,0:T(8,128)(2,1)S(1)}, bf16[256,512]{1,0:T(8,128)(2,1)S(1)}, u32[]{:S(2)}, u32[]{:S(2)}) %collective-permute-start.1) | collective-permute-done | bytes 262176 | tf_op jit(solution)/shard_map/ppermute | solution.py:54
  25.3 1.3 dynamic_slice.24
  27.4 0.8 slice_bitcast_fusion
  28.2 4.7 %collective-permute-done.2 = bf16[256,512]{1,0:T(8,128)(2,1)S(1)} collective-permute-done((bf16[256,512]{1,0:T(8,128)(2,1)S(1)}, bf16[256,512]{1,0:T(8,128)(2,1)S(1)}, u32[]{:S(2)}, u32[]{:S(2)}) %collective-permute-start.2) | collective-permute-done | bytes 262176 | tf_op jit(solution)/shard_map/ppermute | solution.py:54
  32.9 6.7 %fusion.15 = bf16[1024,512]{1,0:T(8,128)(2,1)} fusion(s32[]{:T(128)S(6)} %select_n.56, bf16[256,512]{1,0:T(8,128)(2,1)S(1)} %collective-permute-done.2, bf16[256,512]{1,0:T(8,128)(2,1)S(1)} %collective-permute-done.1, bf16[256,512]{1,0:T(8,128)(2,1)S(1)} %collective-permute-done, bf16[256,512]{1,0:T(8,128)(2,1)} %param.12), kind=kLoop, calls=%fused_computation.47 | loop fusion | flops 8388608 | bytes 2097156 | tf_op jit(solution)/shard_map/jit(_roll_dynamic)/concatenate | solution.py:56
  39.6 2.5 broadcast.46.clone
  42.1 91.4 %while.20 = (s32[]{:T(128)}, f32[16,128,512]{2,1,0:T(8,128)}, s32[]{:T(128)}, s32[128]{0:T(128)S(1)}, s32[]{:T(128)}, /*index=5*/bf16[128,128,128]{2,1,0:T(8,128...) while((s32[]{:T(128)}, f32[16,128,512]{2,1,0:T(8,128)}, ...), condition=%wide.region_2.4_spmd, body=%wide.region_0.3_spmd.sunk | while | flops 270533824 | bytes 23597752 | solution.py:34
  42.2 1.9 gather_fusion
  44.8 3.7 convolution_select_fusion.4
  48.5 8.8 %scatter_fusion = f32[16,128,512]{2,1,0:T(8,128)} fusion(f32[16,128,512]{2,1,0:T(8,128)} %get-tuple-element.254, s32[16]{0:T(128)S(1)} %get-tuple-element.228, f32[16,128,512]{2,1,0:T(8,128)} %convolution_select_fusion.4), kind=kCustom, calls=%fused_computation.2.clone.1 | custom fusion | flops 1048576 | bytes 12582976 | tf_op jit(solution)/shard_map/while/body/scatter-add | solution.py:30
  57.4 1.9 gather_fusion
  59.3 0.7 compare_and_fusion.4
  60.0 3.7 convolution_select_fusion.4
  63.7 8.8 %scatter_fusion = f32[16,128,512]{2,1,0:T(8,128)} fusion(f32[16,128,512]{2,1,0:T(8,128)} %get-tuple-element.254, s32[16]{0:T(128)S(1)} %get-tuple-element.228, f32[16,128,512]{2,1,0:T(8,128)} %convolution_select_fusion.4), kind=kCustom, calls=%fused_computation.2.clone.1 | custom fusion | flops 1048576 | bytes 12582976 | tf_op jit(solution)/shard_map/while/body/scatter-add | solution.py:30
  72.6 1.9 gather_fusion
  74.5 0.7 compare_and_fusion.4
  75.2 3.7 convolution_select_fusion.4
  78.9 8.7 %scatter_fusion = f32[16,128,512]{2,1,0:T(8,128)} fusion(f32[16,128,512]{2,1,0:T(8,128)} %get-tuple-element.254, s32[16]{0:T(128)S(1)} %get-tuple-element.228, f32[16,128,512]{2,1,0:T(8,128)} %convolution_select_fusion.4), kind=kCustom, calls=%fused_computation.2.clone.1 | custom fusion | flops 1048576 | bytes 12582976 | tf_op jit(solution)/shard_map/while/body/scatter-add | solution.py:30
  87.7 1.9 gather_fusion
  89.6 0.7 compare_and_fusion.4
  90.3 3.7 convolution_select_fusion.4
  94.0 8.9 %scatter_fusion = f32[16,128,512]{2,1,0:T(8,128)} fusion(f32[16,128,512]{2,1,0:T(8,128)} %get-tuple-element.254, s32[16]{0:T(128)S(1)} %get-tuple-element.228, f32[16,128,512]{2,1,0:T(8,128)} %convolution_select_fusion.4), kind=kCustom, calls=%fused_computation.2.clone.1 | custom fusion | flops 1048576 | bytes 12582976 | tf_op jit(solution)/shard_map/while/body/scatter-add | solution.py:30
  102.9 1.9 gather_fusion
  105.6 3.7 convolution_select_fusion.4
  109.2 8.9 %scatter_fusion = f32[16,128,512]{2,1,0:T(8,128)} fusion(f32[16,128,512]{2,1,0:T(8,128)} %get-tuple-element.254, s32[16]{0:T(128)S(1)} %get-tuple-element.228, f32[16,128,512]{2,1,0:T(8,128)} %convolution_select_fusion.4), kind=kCustom, calls=%fused_computation.2.clone.1 | custom fusion | flops 1048576 | bytes 12582976 | tf_op jit(solution)/shard_map/while/body/scatter-add | solution.py:30
  118.2 1.9 gather_fusion
  120.8 3.7 convolution_select_fusion.4
  124.5 9.0 %scatter_fusion = f32[16,128,512]{2,1,0:T(8,128)} fusion(f32[16,128,512]{2,1,0:T(8,128)} %get-tuple-element.254, s32[16]{0:T(128)S(1)} %get-tuple-element.228, f32[16,128,512]{2,1,0:T(8,128)} %convolution_select_fusion.4), kind=kCustom, calls=%fused_computation.2.clone.1 | custom fusion | flops 1048576 | bytes 12582976 | tf_op jit(solution)/shard_map/while/body/scatter-add | solution.py:30
  133.6 81.5 %reduce-scatter.3.cloned.1.call-done = f32[256,512]{1,0:T(8,128)} async-done(((f32[2048,512]{1,0:T(8,128)}), f32[256,512]{1,0:T(8,128)}) %reduce-scatter.3.cloned.1.call-update) | async-done | bytes 524304 | tf_op jit(solution)/shard_map/reduce_scatter | solution.py:64
  215.1 2.1 fusion.4
  217.2 1.5 collective-permute-start.3
  218.7 5.8 %collective-permute-done.3 = bf16[256,512]{1,0:T(8,128)(2,1)S(1)} collective-permute-done((bf16[256,512]{1,0:T(8,128)(2,1)S(1)}, bf16[256,512]{1,0:T(8,128)(2,1)S(1)}, u32[]{:S(2)}, u32[]{:S(2)}) %collective-permute-start.3) | collective-permute-done | bytes 262176 | tf_op jit(solution)/shard_map/ppermute | solution.py:54
  224.6 1.1 collective-permute-start.4
  225.7 7.0 %collective-permute-done.4 = bf16[256,512]{1,0:T(8,128)(2,1)S(1)} collective-permute-done((bf16[256,512]{1,0:T(8,128)(2,1)S(1)}, bf16[256,512]{1,0:T(8,128)(2,1)S(1)}, u32[]{:S(2)}, u32[]{:S(2)}) %collective-permute-start.4) | collective-permute-done | bytes 262176 | tf_op jit(solution)/shard_map/ppermute | solution.py:54
  232.7 1.1 collective-permute-start.5
  233.8 6.2 %collective-permute-done.5 = bf16[256,512]{1,0:T(8,128)(2,1)S(1)} collective-permute-done((bf16[256,512]{1,0:T(8,128)(2,1)S(1)}, bf16[256,512]{1,0:T(8,128)(2,1)S(1)}, u32[]{:S(2)}, u32[]{:S(2)}) %collective-permute-start.5) | collective-permute-done | bytes 262176 | tf_op jit(solution)/shard_map/ppermute | solution.py:54
  239.9 6.9 %fusion.8 = bf16[1024,512]{1,0:T(8,128)(2,1)} fusion(s32[]{:T(128)S(6)} %select_n.56, bf16[256,512]{1,0:T(8,128)(2,1)S(1)} %collective-permute-done.5, bf16[256,512]{1,0:T(8,128)(2,1)S(1)} %collective-permute-done.4, bf16[256,512]{1,0:T(8,128)(2,1)S(1)} %collective-permute-done.3, bf16[256,512]{1,0:T(8,128)(2,1)S(1)} %fusion.4), kind=kLoop, calls=%fused_computation.40 | loop fusion | flops 8388608 | bytes 2097156 | tf_op jit(solution)/shard_map/jit(_roll_dynamic)/concatenate | solution.py:56
  246.8 2.5 broadcast.46
  249.3 91.4 %while.21 = (s32[]{:T(128)}, f32[16,128,512]{2,1,0:T(8,128)}, s32[]{:T(128)}, s32[128]{0:T(128)S(1)}, s32[]{:T(128)}, /*index=5*/bf16[128,128,128]{2,1,0:T(8,128...) while((s32[]{:T(128)}, f32[16,128,512]{2,1,0:T(8,128)}, ...), condition=%wide.region_6.8_spmd, body=%wide.region_4.7_spmd.sunk | while | flops 270533824 | bytes 23597752 | solution.py:34
  249.4 1.9 gather_fusion.1
  251.3 0.7 compare_and_fusion.5
  252.0 3.7 convolution_select_fusion.5
  255.7 8.8 %scatter_fusion.1 = f32[16,128,512]{2,1,0:T(8,128)} fusion(f32[16,128,512]{2,1,0:T(8,128)} %get-tuple-element.293, s32[16]{0:T(128)S(1)} %get-tuple-element.238, f32[16,128,512]{2,1,0:T(8,128)} %convolution_select_fusion.5), kind=kCustom, calls=%fused_computation.3.clone.1 | custom fusion | flops 1048576 | bytes 12582976 | tf_op jit(solution)/shard_map/while/body/scatter-add | solution.py:30
  264.6 1.9 gather_fusion.1
  267.3 3.7 convolution_select_fusion.5
  270.9 8.8 %scatter_fusion.1 = f32[16,128,512]{2,1,0:T(8,128)} fusion(f32[16,128,512]{2,1,0:T(8,128)} %get-tuple-element.293, s32[16]{0:T(128)S(1)} %get-tuple-element.238, f32[16,128,512]{2,1,0:T(8,128)} %convolution_select_fusion.5), kind=kCustom, calls=%fused_computation.3.clone.1 | custom fusion | flops 1048576 | bytes 12582976 | tf_op jit(solution)/shard_map/while/body/scatter-add | solution.py:30
  279.8 1.9 gather_fusion.1
  282.4 3.7 convolution_select_fusion.5
  286.1 8.7 %scatter_fusion.1 = f32[16,128,512]{2,1,0:T(8,128)} fusion(f32[16,128,512]{2,1,0:T(8,128)} %get-tuple-element.293, s32[16]{0:T(128)S(1)} %get-tuple-element.238, f32[16,128,512]{2,1,0:T(8,128)} %convolution_select_fusion.5), kind=kCustom, calls=%fused_computation.3.clone.1 | custom fusion | flops 1048576 | bytes 12582976 | tf_op jit(solution)/shard_map/while/body/scatter-add | solution.py:30
  294.9 1.9 gather_fusion.1
  296.8 0.7 compare_and_fusion.5
  297.5 3.7 convolution_select_fusion.5
  301.2 8.9 %scatter_fusion.1 = f32[16,128,512]{2,1,0:T(8,128)} fusion(f32[16,128,512]{2,1,0:T(8,128)} %get-tuple-element.293, s32[16]{0:T(128)S(1)} %get-tuple-element.238, f32[16,128,512]{2,1,0:T(8,128)} %convolution_select_fusion.5), kind=kCustom, calls=%fused_computation.3.clone.1 | custom fusion | flops 1048576 | bytes 12582976 | tf_op jit(solution)/shard_map/while/body/scatter-add | solution.py:30
  310.2 1.9 gather_fusion.1
  312.8 3.7 convolution_select_fusion.5
  316.5 8.9 %scatter_fusion.1 = f32[16,128,512]{2,1,0:T(8,128)} fusion(f32[16,128,512]{2,1,0:T(8,128)} %get-tuple-element.293, s32[16]{0:T(128)S(1)} %get-tuple-element.238, f32[16,128,512]{2,1,0:T(8,128)} %convolution_select_fusion.5), kind=kCustom, calls=%fused_computation.3.clone.1 | custom fusion | flops 1048576 | bytes 12582976 | tf_op jit(solution)/shard_map/while/body/scatter-add | solution.py:30
  325.4 1.9 gather_fusion.1
  328.1 3.7 convolution_select_fusion.5
  331.7 9.0 %scatter_fusion.1 = f32[16,128,512]{2,1,0:T(8,128)} fusion(f32[16,128,512]{2,1,0:T(8,128)} %get-tuple-element.293, s32[16]{0:T(128)S(1)} %get-tuple-element.238, f32[16,128,512]{2,1,0:T(8,128)} %convolution_select_fusion.5), kind=kCustom, calls=%fused_computation.3.clone.1 | custom fusion | flops 1048576 | bytes 12582976 | tf_op jit(solution)/shard_map/while/body/scatter-add | solution.py:30
  340.8 83.4 %reduce-scatter.5.cloned.1.call-done = f32[256,512]{1,0:T(8,128)} async-done(((f32[2048,512]{1,0:T(8,128)}), f32[256,512]{1,0:T(8,128)}) %reduce-scatter.5.cloned.1.call-update) | async-done | bytes 524304 | tf_op jit(solution)/shard_map/reduce_scatter | solution.py:64
  424.2 2.9 convolution_maximum_fusion
  (40 shorter events, 6.0 us)
Async XLA Ops:
  6.5 208.6 %copy-start = (f32[512,512]{1,0:T(8,128)S(1)}, f32[512,512]{1,0:T(8,128)}, u32[]{:S(2)}) copy-start(f32[512,512]{1,0:T(8,128)} %param.16) | copy-start | bytes 3145732
  6.5 208.6 %reduce-scatter.3.cloned.1.call-start = ((), (), s32[]{:S(2)}) async-start(), calls=%async_computation.2 | async-start | bytes 4718592 | tf_op jit(solution)/shard_map/reduce_scatter | solution.py:64
  6.5 10.4 %collective-permute-start = (bf16[256,512]{1,0:T(8,128)(2,1)}, bf16[256,512]{1,0:T(8,128)(2,1)S(1)}, u32[]{:S(2)}, u32[]{:S(2)}) collective-permute-start(bf16[256,512]{1,0:T(8,128)(2,1)} %param.12), channel_id=1, source_target_pairs={{0,8},{8,16},{16,24},{24,0},{1,9},{9,17},{17,25},{25,1},{2,10},{10... | collective-permute-start | bytes 786440 | tf_op jit(solution)/shard_map/ppermute | solution.py:54
  17.0 8.4 %collective-permute-start.1 = (bf16[256,512]{1,0:T(8,128)(2,1)S(1)}, bf16[256,512]{1,0:T(8,128)(2,1)S(1)}, u32[]{:S(2)}, u32[]{:S(2)}) collective-permute-start(bf16[256,512]{1,0:T(8,128)(2,1)S(1)} %collective-permute-done), channel_id=1, source_target_pairs={{0,8},{8,16},{16,24},{24,0},{1,9},{9,17},{17,25},{25,1},{2,10},{10... | collective-permute-start | bytes 786440 | tf_op jit(solution)/shard_map/ppermute | solution.py:54
  25.3 7.5 %collective-permute-start.2 = (bf16[256,512]{1,0:T(8,128)(2,1)S(1)}, bf16[256,512]{1,0:T(8,128)(2,1)S(1)}, u32[]{:S(2)}, u32[]{:S(2)}) collective-permute-start(bf16[256,512]{1,0:T(8,128)(2,1)S(1)} %collective-permute-done.1), channel_id=1, source_target_pairs={{0,8},{8,16},{16,24},{24,0},{1,9},{9,17},{17,25},{25,1},{2,10},{10... | collective-permute-start | bytes 786440 | tf_op jit(solution)/shard_map/ppermute | solution.py:54
  133.6 290.6 %reduce-scatter.5.cloned.1.call-start = ((), (), s32[]{:S(2)}) async-start(), calls=%async_computation.3 | async-start | bytes 4718592 | tf_op jit(solution)/shard_map/reduce_scatter | solution.py:64
  217.2 7.3 %collective-permute-start.3 = (bf16[256,512]{1,0:T(8,128)(2,1)S(1)}, bf16[256,512]{1,0:T(8,128)(2,1)S(1)}, u32[]{:S(2)}, u32[]{:S(2)}) collective-permute-start(bf16[256,512]{1,0:T(8,128)(2,1)S(1)} %fusion.4), channel_id=1, source_target_pairs={{0,8},{8,16},{16,24},{24,0},{1,9},{9,17},{17,25},{25,1},{2,10},{10... | collective-permute-start | bytes 786440 | tf_op jit(solution)/shard_map/ppermute | solution.py:54
  224.6 8.1 %collective-permute-start.4 = (bf16[256,512]{1,0:T(8,128)(2,1)S(1)}, bf16[256,512]{1,0:T(8,128)(2,1)S(1)}, u32[]{:S(2)}, u32[]{:S(2)}) collective-permute-start(bf16[256,512]{1,0:T(8,128)(2,1)S(1)} %collective-permute-done.3), channel_id=1, source_target_pairs={{0,8},{8,16},{16,24},{24,0},{1,9},{9,17},{17,25},{25,1},{2,10},{10... | collective-permute-start | bytes 786440 | tf_op jit(solution)/shard_map/ppermute | solution.py:54
  232.7 7.3 %collective-permute-start.5 = (bf16[256,512]{1,0:T(8,128)(2,1)S(1)}, bf16[256,512]{1,0:T(8,128)(2,1)S(1)}, u32[]{:S(2)}, u32[]{:S(2)}) collective-permute-start(bf16[256,512]{1,0:T(8,128)(2,1)S(1)} %collective-permute-done.4), channel_id=1, source_target_pairs={{0,8},{8,16},{16,24},{24,0},{1,9},{9,17},{17,25},{25,1},{2,10},{10... | collective-permute-start | bytes 786440 | tf_op jit(solution)/shard_map/ppermute | solution.py:54
  340.8 83.4 %copy-start.1 = (f32[512,512]{1,0:T(8,128)S(1)}, f32[512,512]{1,0:T(8,128)}, u32[]{:S(2)}) copy-start(f32[512,512]{1,0:T(8,128)} %param.17) | copy-start | bytes 3145732
Sparse Core Ops, SparseCore 0:
  133.7 81.3 reduce-scatter.2
  340.9 83.1 reduce-scatter.4
